TPU v7x, 32 devices: a whole 2x2x4 slice. The times are simulated.
32 devices in a mesh: seq: 16 (over z, x, core), row: 2 (over y).
Axes of the slice: x: 2, y: 2, z: 4, core: 2. Of those that a mesh axis runs over, the one named last changes fastest.
Arguments:
- patch_queries: bfloat16 [2048, 2048], P('seq', 'row'), may hold values from -15 to 15
- patch_keys: bfloat16 [2048, 2048], P('seq', 'row'), may hold values from -15 to 15
- patch_values: bfloat16 [2048, 2048], P('seq', 'row'), may hold values from -6 to 6
- patch_tasks: int32 [2048], P('seq'), may hold values from 0 to 7
- residual: bfloat16 [2048, 2048], P('seq', 'row'), may hold values from -6 to 6
- output_weight: bfloat16 [2048, 2048], P('row'), may hold values from -0.5 to 0.5
- global_down: bfloat16 [2048, 16], P('row'), may hold values from -0.5 to 0.5
- global_up: bfloat16 [16, 2048], P(None, 'row'), may hold values from -1.5 to 1.5
- global_scales: float32 [8, 16], replicated, may hold values from 0.25 to 4
- local_weight: bfloat16 [2048, 512], P('row'), may hold values from -0.125 to 0.125
- byte_ids: int32 [16384], P('seq'), may hold values from 0 to 255
- byte_table: bfloat16 [256, 512], replicated, may hold values from -6 to 6
- position_table: bfloat16 [8, 512], replicated, may hold values from -6 to 6
- norm_gain: float32 [512], replicated, may hold values from 0.5 to 1.5
- hidden_in: bfloat16 [2048, 512], P('row', 'seq'), may hold values from -0.25 to 0.25
- hidden_out: bfloat16 [2048, 512], P('row', 'seq'), may hold values from -0.125 to 0.125
- local_down: bfloat16 [512, 16], replicated, may hold values from -0.25 to 0.25
- local_up: bfloat16 [16, 2048], P(None, 'row'), may hold values from -1.5 to 1.5
- local_scales: float32 [8, 16], replicated, may hold values from 0.25 to 4
- cotangent: bfloat16 [16384, 512], P(('seq', 'row')), may hold values from -6 to 6
Outputs:
- grad_global_down: float32 [2048, 16], P('row')
- grad_global_up: float32 [16, 2048], P(None, 'row')
- grad_global_scales: float32 [8, 16], replicated
- grad_local_down: float32 [512, 16], replicated
- grad_local_up: float32 [16, 2048], P(None, 'row')
- grad_local_scales: float32 [8, 16], replicated
All inputs are finite; a program needn't handle non-finite values.
Results may differ from a plain program's by a relative error of at most 0.028.
Values may be sent and summed in bfloat16 or wider, within the bound.
A program may use at most 64 MiB of HBM per device.

v0:
```python
import math

import jax
import jax.numpy as jnp
from jax import lax
from jax.sharding import PartitionSpec as P

HEAD = 128
VOCAB = 256
PATCH = 8
TASKS = 8


def contract(left, right, left_dim, right_dim):
    return lax.dot_general(
        left, right, (((left_dim,), (right_dim,)), ((), ())), preferred_element_type=jnp.float32
    )


def select_rows(table, tasks):
    picks = (tasks[:, None] == jnp.arange(table.shape[0], dtype=jnp.int32)[None, :]).astype(
        jnp.float32
    )
    return jnp.dot(picks, table, precision=lax.Precision.HIGHEST)


def task_totals(tasks, values):
    picks = (tasks[:, None] == jnp.arange(TASKS, dtype=jnp.int32)[None, :]).astype(jnp.float32)
    return lax.dot_general(picks, values, (((0,), (0,)), ((), ())), precision=lax.Precision.HIGHEST)


def gelu_slope(upper):
    cumulative = 0.5 * (1.0 + lax.erf(upper * 0.7071067811865476))
    density = jnp.exp(-0.5 * upper * upper) * 0.3989422804014327
    return cumulative + upper * density


def local_inputs(
    identities, projected, tasks, byte_table, position_table, norm_gain, local_down, local_scales
):
    count = identities.shape[0]
    picks = (identities[:, None] == jnp.arange(VOCAB, dtype=jnp.int32)[None, :]).astype(
        jnp.bfloat16
    )
    embedded = jnp.dot(picks, byte_table, preferred_element_type=jnp.float32)
    patches = count // PATCH
    inputs = (
        embedded.reshape(patches, PATCH, -1)
        + position_table.astype(jnp.float32)[None]
        + projected.astype(jnp.float32)[:, None, :]
    )
    inputs = inputs.reshape(count, -1)
    inverse = lax.rsqrt(jnp.mean(inputs * inputs, axis=1, keepdims=True) + 1e-06)
    normed = (inputs * inverse * norm_gain).astype(jnp.bfloat16)
    lowered = jnp.dot(normed, local_down, preferred_element_type=jnp.float32)
    byte_tasks = jnp.repeat(tasks, PATCH)
    scales = select_rows(local_scales, byte_tasks)
    shrunk = (lowered * scales).astype(jnp.bfloat16)
    return (inputs, inverse, normed, lowered, scales, shrunk, byte_tasks)


def keep_state(current):
    return current


def update_state(state, query_rows, first, key_heads, value_heads, key_places, scale):
    running_max, running_sum, running_out = state
    count = query_rows.shape[0]
    heads = key_heads.shape[1]
    query_heads = query_rows.reshape(count, heads, HEAD)
    scores = (
        jnp.einsum("qhd,khd->hqk", query_heads, key_heads, preferred_element_type=jnp.float32)
        * scale
    )
    query_places = first + jnp.arange(count, dtype=jnp.int32)
    allowed = key_places[None, :] <= query_places[:, None]
    scores = jnp.where(allowed[None], scores, -1e30)
    new_max = jnp.maximum(running_max, jnp.max(scores, axis=2))
    weights = jnp.where(allowed[None], jnp.exp(scores - new_max[:, :, None]), 0.0)
    shrink = jnp.exp(running_max - new_max)
    running_sum = running_sum * shrink + jnp.sum(weights, axis=2)
    mixed = jnp.einsum(
        "hqk,khd->qhd",
        weights.astype(jnp.bfloat16),
        value_heads,
        preferred_element_type=jnp.float32,
    )
    running_out = running_out * jnp.transpose(shrink)[:, :, None] + mixed
    return (new_max, running_sum, running_out)


def finish_state(state):
    running_max, running_sum, running_out = state
    result = running_out / jnp.transpose(running_sum)[:, :, None]
    return result.reshape(result.shape[0], -1).astype(jnp.bfloat16)


def body(
    patch_queries,
    patch_keys,
    patch_values,
    patch_tasks,
    residual,
    output_weight,
    global_down,
    global_up,
    global_scales,
    local_weight,
    byte_ids,
    byte_table,
    position_table,
    norm_gain,
    hidden_in,
    hidden_out,
    local_down,
    local_up,
    local_scales,
    cotangent,
):
    rows = patch_queries.shape[0]
    width = patch_queries.shape[1]
    heads = width // HEAD
    row_count = lax.axis_size("row")
    seq_index = lax.axis_index("seq")
    row_index = lax.axis_index("row")
    scale = 1.0 / math.sqrt(HEAD)
    own_first = seq_index * rows
    groups = [(patch_queries, own_first)]

    def visit(state, query_rows, first, key_heads, value_heads, key_places):

        def refresh(current):
            return update_state(
                current, query_rows, first, key_heads, value_heads, key_places, scale
            )

        return lax.cond(
            key_places[0] <= first + query_rows.shape[0] - 1, refresh, keep_state, state
        )

    initial = tuple(
        (
            (
                jnp.full((heads, query_rows.shape[0]), -1e30, jnp.float32),
                jnp.zeros((heads, query_rows.shape[0]), jnp.float32),
                jnp.zeros((query_rows.shape[0], heads, HEAD), jnp.float32),
            )
            for query_rows, first in groups
        )
    )
    key_piece = lax.all_gather(patch_keys, "seq", axis=0, tiled=True)
    value_piece = lax.all_gather(patch_values, "seq", axis=0, tiled=True)
    count = key_piece.shape[0]
    span = math.gcd(count, 1024)

    def one_span(index, states):
        offset = index * span
        key_heads = lax.dynamic_slice_in_dim(key_piece, offset, span, 0).reshape(span, heads, HEAD)
        value_heads = lax.dynamic_slice_in_dim(value_piece, offset, span, 0).reshape(
            span, heads, HEAD
        )
        key_places = offset + jnp.arange(span, dtype=jnp.int32)
        updated = []
        for (query_rows, first), state in zip(groups, states):
            updated.append(visit(state, query_rows, first, key_heads, value_heads, key_places))
        return tuple(updated)

    states = lax.fori_loop(0, count // span, one_span, initial)
    outputs = [finish_state(state) for state in states]
    attended = outputs[0]
    reduced = lax.psum(jnp.dot(attended, global_down, preferred_element_type=jnp.float32), "row")
    task_scales = select_rows(global_scales, patch_tasks)
    scaled = (reduced * task_scales).astype(jnp.bfloat16)
    mixed = lax.psum_scatter(
        contract(output_weight, attended, 0, 1).astype(jnp.bfloat16),
        "row",
        scatter_dimension=0,
        tiled=True,
    ).astype(jnp.float32)
    mixed = mixed + jnp.transpose(residual.astype(jnp.float32)) + contract(global_up, scaled, 0, 1)
    mixed_b = mixed.astype(jnp.bfloat16)
    own_patches = rows // row_count
    own_bytes = own_patches * PATCH
    rows_in, rows_out = (
        lax.all_gather(hidden_in, "seq", axis=1, tiled=True),
        lax.all_gather(hidden_out, "seq", axis=1, tiled=True),
    )
    partial_value = contract(mixed_b, local_weight, 0, 0)
    projected = lax.psum(partial_value.astype(jnp.bfloat16), "row")
    every = local_inputs(
        byte_ids,
        projected,
        patch_tasks,
        byte_table,
        position_table,
        norm_gain,
        local_down,
        local_scales,
    )
    normed_all = every[2]
    shrunk_all = every[5]
    cotangent_all = lax.all_gather(cotangent, "row", axis=0, tiled=True)
    inputs, inverse, normed, lowered, scales, shrunk, byte_tasks = [
        lax.dynamic_slice_in_dim(value, row_index * own_bytes, own_bytes, 0) for value in every
    ]
    upper = contract(normed_all, rows_in, 1, 1) + jnp.dot(
        shrunk_all, local_up, preferred_element_type=jnp.float32
    )
    through = contract(cotangent_all, rows_out, 1, 1)
    grown = (through * gelu_slope(upper)).astype(jnp.bfloat16)
    grad_local_up = contract(shrunk_all, grown, 0, 0)
    back_norm, back_rank = (
        lax.psum_scatter(
            jnp.dot(grown, rows_in, preferred_element_type=jnp.float32).astype(jnp.bfloat16),
            "row",
            scatter_dimension=0,
            tiled=True,
        ).astype(jnp.float32),
        lax.psum_scatter(
            contract(grown, local_up, 1, 1).astype(jnp.bfloat16),
            "row",
            scatter_dimension=0,
            tiled=True,
        ).astype(jnp.float32),
    )
    grad_local_scales = task_totals(byte_tasks, back_rank * lowered)
    moved = (back_rank * scales).astype(jnp.bfloat16)
    grad_local_down = contract(normed, moved, 0, 0)
    back_total = back_norm + contract(moved, local_down, 1, 1)
    gained = back_total * norm_gain
    average = jnp.mean(gained * inputs, axis=1, keepdims=True)
    back_inputs = cotangent.astype(jnp.float32) + inverse * (
        gained - inputs * inverse * inverse * average
    )
    patch_grad = back_inputs.reshape(own_patches, PATCH, -1).sum(axis=1).astype(jnp.bfloat16)
    back_mixed = contract(
        lax.all_gather(patch_grad, "row", axis=0, tiled=True), local_weight, 1, 1
    ).astype(jnp.bfloat16)
    grad_global_up = contract(scaled, back_mixed, 0, 0)
    back_scaled = lax.psum(contract(back_mixed, global_up, 1, 1), "row")
    grad_global_scales = task_totals(patch_tasks, back_scaled * reduced)
    back_reduced = (back_scaled * task_scales).astype(jnp.bfloat16)
    grad_global_down = contract(attended, back_reduced, 0, 0)
    grad_global_down, grad_global_up, grad_global_scales, grad_local_up = lax.psum(
        (grad_global_down, grad_global_up, grad_global_scales, grad_local_up), "seq"
    )
    grad_local_down, grad_local_scales = lax.psum(
        (grad_local_down, grad_local_scales), ("seq", "row")
    )
    return (
        grad_global_down,
        grad_global_up,
        grad_global_scales,
        grad_local_down,
        grad_local_up,
        grad_local_scales,
    )


def solution(mesh):
    placed = (
        P("seq", "row"),
        P("seq", "row"),
        P("seq", "row"),
        P("seq"),
        P("seq", "row"),
        P("row", None),
        P("row", None),
        P(None, "row"),
        P(),
        P("row", None),
        P("seq"),
        P(),
        P(),
        P(),
        P("row", "seq"),
        P("row", "seq"),
        P(),
        P(None, "row"),
        P(),
        P(("seq", "row"), None),
    )
    return jax.shard_map(
        body,
        mesh=mesh,
        in_specs=placed,
        out_specs=(P("row", None), P(None, "row"), P(), P(), P(None, "row"), P()),
        check_vma=False,
    )
```

profile of v0, /device:TPU:0, one launch (start us, length us, event | category | flops | bytes accessed | tf_op | source)
XLA Modules:
  0.0 456.6 jit_solution(17964355863576185190)
XLA Ops:
  7.2 1.9 copy.32
  9.2 1.8 copy.33
  11.1 54.3 %all-gather.6.cloned.1.call-done = bf16[2048,1024]{0,1:T(8,128)(2,1)} async-done(((bf16[128,1024]{0,1:T(8,128)(2,1)}), bf16[2048,1024]{0,1:T(8,128)(2,1)}) %all-gather.6.cloned.1.call-update) | async-done | bytes 4194320 | tf_op jit(solution)/shard_map/all_gather | solution.py:151
  65.4 52.8 %all-gather.8.cloned.1.call-done = bf16[2048,1024]{0,1:T(8,128)(2,1)} async-done(((bf16[128,1024]{0,1:T(8,128)(2,1)}), bf16[2048,1024]{0,1:T(8,128)(2,1)}) %all-gather.8.cloned.1.call-update) | async-done | bytes 4194320 | tf_op jit(solution)/shard_map/all_gather | solution.py:152
  118.3 9.3 %while.19 = (s32[]{:T(128)}, f32[8,128]{1,0:T(8,128)S(1)}, f32[8,128]{1,0:T(8,128)S(1)}, f32[128,8,128]{2,0,1:T(8,128)S(1)}, s32[]{:T(128)}, /*index=5*/s32[]{:T...) while((s32[]{:T(128)}, f32[8,128]{1,0:T(8,128)S(1)}, ...), condition=%wide.region_5.6_spmd, body=%wide.region_0.5_spmd.sunk | while | flops 550899840 | bytes 28124504 | solution.py:168
  118.3 0.5 slice.10
  119.5 6.9 %conditional.2 = ((f32[8,128]{1,0:T(8,128)S(1)}, f32[8,128]{1,0:T(8,128)S(1)}, f32[128,8,128]{2,0,1:T(8,128)S(1)})) conditional(s32[]{:T(128)} %convert_element_type.155, (f32[8,128]{1,0:T(8,128)S(1)}, f32[8,128]{1,0:T(8,128)S(1)}, f32[128,8,128]{2,0,1:T(8,128)S(1)}) %tuple.65, (s32[1024]{0:T(1024)S(1)}, s32[]{:T(128)}, s32[]{:T(128)}, ...), branch_computations={%region_1.0_spmd, %region_2.4_spmd} | conditional | flops 550898816 | bytes 28120166 | solution.py:137
  119.5 2.7 constant_dynamic-slice_fusion
  122.3 0.2 broadcast_compare_fusion
  122.5 1.1 fusion
  123.6 1.7 fusion.13
  125.3 1.0 fusion.2
  126.4 0.5 slice.10
  127.7 0.2 copy.34
  127.9 0.1 divide_convert_fusion
  128.0 3.7 fusion.29
  131.8 0.5 all-gather.10.cloned.1.call-update
  132.4 0.5 all-gather.12.cloned.1.call-update
  133.0 0.2 fusion.65
  133.1 5.0 %psum.63 = f32[128,16]{0,1:T(8,128)S(1)} all-reduce(f32[128,16]{0,1:T(8,128)S(1)} %fusion.65), channel_id=1, replica_groups=mesh['seq'=16,'row'=2] {'row'}, use_global_device_ids=true, to_apply=%region_7.8 | all-reduce | flops 2048 | bytes 16384 | tf_op jit(solution)/shard_map/psum | solution.py:171
  138.1 0.8 multiply_convert_fusion.3
  139.0 12.6 %reduce-scatter.4.cloned.1.call-done = bf16[1024,128]{0,1:T(8,128)(2,1)} async-done(((bf16[2048,128]{0,1:T(8,128)(2,1)}), bf16[1024,128]{0,1:T(8,128)(2,1)}) %reduce-scatter.4.cloned.1.call-update) | async-done | bytes 262160 | tf_op jit(solution)/shard_map/reduce_scatter | solution.py:174
  151.6 2.1 fusion.34
  153.7 0.7 all-gather.14.cloned.1.call-update
  154.5 0.1 eq.29
  154.6 0.1 eq.32
  154.7 0.5 fusion.40
  155.2 19.1 %all-gather.10.cloned.1.call-done = bf16[1024,512]{1,0:T(8,128)(2,1)} async-done(((bf16[512,512]{1,0:T(8,128)(2,1)}), bf16[1024,512]{1,0:T(8,128)(2,1)}) %all-gather.10.cloned.1.call-update) | async-done | bytes 1048592 | tf_op jit(solution)/shard_map/all_gather | solution.py:202
  174.3 39.9 %all-gather.12.cloned.1.call-done = bf16[1024,512]{0,1:T(8,128)(2,1)} async-done(((bf16[1024,32]{0,1:T(8,128)(2,1)}), bf16[1024,512]{0,1:T(8,128)(2,1)}) %all-gather.12.cloned.1.call-update) | async-done | bytes 1048592 | tf_op jit(solution)/shard_map/all_gather | solution.py:186
  214.2 4.7 %fusion.60 = f32[1024,1024]{1,0:T(8,128)} fusion(bf16[1024,512]{1,0:T(8,128)(2,1)} %all-gather.10.cloned.1.call-done, bf16[1024,512]{0,1:T(8,128)(2,1)} %all-gather.12.cloned.1.call-done), kind=kOutput, calls=%fused_computation.86 | convolution fusion | flops 1073741824 | bytes 6291456 | tf_op jit(solution)/shard_map/dot_general | solution.py:15
  218.9 17.9 %all-reduce.5.cloned.1.call-done = bf16[128,512]{1,0:T(8,128)(2,1)} async-done(((bf16[128,512]{1,0:T(8,128)(2,1)}), bf16[128,512]{1,0:T(8,128)(2,1)}) %all-reduce.5.cloned.1.call-update) | async-done | bytes 131088 | tf_op jit(solution)/shard_map/psum | solution.py:189
  236.8 0.9 convert_element_type.97
  237.7 1.6 multiply_reduce_fusion
  239.4 0.6 copy-done.9
  240.0 0.2 multiply_convert_fusion
  240.2 1.0 copy-done.3
  241.2 1.0 multiply_convert_fusion.1
  242.3 34.6 %all-gather.14.cloned.1.call-done = bf16[1024,512]{0,1:T(8,128)(2,1)} async-done(((bf16[1024,32]{0,1:T(8,128)(2,1)}), bf16[1024,512]{0,1:T(8,128)(2,1)}) %all-gather.14.cloned.1.call-update) | async-done | bytes 1048592 | tf_op jit(solution)/shard_map/all_gather | solution.py:185
  276.8 2.9 fusion.61
  279.8 2.3 fusion.28
  282.1 1.3 copy-done.1
  283.4 1.3 convolution_convert_fusion.3
  284.7 0.2 reduce-scatter.6.cloned.1.call-start
  284.9 4.1 convolution_convert_fusion.1
  289.2 1.3 dynamic_slice.47
  290.5 1.3 dynamic-slice.3
  291.8 2.6 fusion.64
  294.4 1.8 fusion.43
  296.2 1.2 fusion.36
  297.4 40.2 %all-reduce = (f32[512,16]{0,1:T(8,128)}, f32[8,16]{1,0:T(8,128)}) all-reduce(f32[512,16]{0,1:T(8,128)S(1)} %fusion.36, f32[8,16]{1,0:T(8,128)} %fusion.43), channel_id=1, replica_groups=mesh['seq'=16,'row'=2] {'seq','row'}, use_global_device_ids=true, to_apply=%region_18.19 | all-reduce | flops 8320 | bytes 66560 | tf_op jit(solution)/shard_map/psum | solution.py:247
  337.7 1.5 multiply_reduce_fusion.1
  339.2 1.6 bitcast_reduce_fusion
  340.8 5.2 %all_gather.23 = bf16[128,512]{1,0:T(8,128)(2,1)S(1)} all-gather(bf16[64,512]{1,0:T(8,128)(2,1)S(1)} %bitcast_reduce_fusion), channel_id=1, replica_groups=mesh['seq'=16,'row'=2] {'row'}, dimensions={0}, use_global_device_ids=true | all-gather | bytes 196608 | tf_op jit(solution)/shard_map/all_gather | solution.py:237
  346.0 0.5 convolution_convert_fusion.2
  346.5 0.2 fusion.62
  346.7 0.8 fusion.63
  347.5 5.0 %psum.65 = f32[128,16]{0,1:T(8,128)S(1)} all-reduce(f32[128,16]{0,1:T(8,128)S(1)} %fusion.62), channel_id=1, replica_groups=mesh['seq'=16,'row'=2] {'row'}, use_global_device_ids=true, to_apply=%region_14.15 | all-reduce | flops 2048 | bytes 16384 | tf_op jit(solution)/shard_map/psum | solution.py:240
  352.4 0.8 fusion.55
  353.3 0.2 fusion.49
  353.5 30.1 %psum.68 = f32[8,16]{1,0:T(8,128)} all-reduce(f32[8,16]{1,0:T(8,128)S(1)} %fusion.49), channel_id=1, replica_groups=mesh['seq'=16,'row'=2] {'seq'}, use_global_device_ids=true, to_apply=%region_17.18 | all-reduce | flops 128 | bytes 1024 | tf_op jit(solution)/shard_map/psum | solution.py:244
  383.6 61.7 %all-reduce.7.cloned.1.call-done = (f32[1024,16]{0,1:T(8,128)}, f32[16,1024]{1,0:T(8,128)}, f32[16,1024]{1,0:T(8,128)}) async-done(((f32[1024,16]{0,1:T(8,128)}, f32[16,1024]{1,0:T(8,128)}, f32[16,1024]{1,0:T(8,128)}), (f32[1024,16]{0,1:T(8,128)}, f32[16,1024]{1,0:T(8,128)}, f32[16,1024]{1,0:T(8,128)})) %all-reduce.7.cloned.1.call-update) | async-done | bytes 196624 | tf_op jit(solution)/shard_map/psum | solution.py:244
  445.3 1.5 copy.67
  446.8 1.5 copy.68
  448.3 1.5 copy.69
  (74 shorter events, 0.7 us)
Async XLA Ops:
  7.2 144.4 %copy-start = (bf16[1024,512]{1,0:T(8,128)(2,1)S(1)}, bf16[1024,512]{1,0:T(8,128)(2,1)}, u32[]{:S(2)}) copy-start(bf16[1024,512]{1,0:T(8,128)(2,1)} %param.33) | copy-start | bytes 3145732
  7.2 58.2 %all-gather.6.cloned.1.call-start = ((), (), s32[]{:S(2)}) async-start(), calls=%async_computation.3 | async-start | bytes 4456448 | tf_op jit(solution)/shard_map/all_gather | solution.py:151
  9.1 109.1 %all-gather.8.cloned.1.call-start = ((), (), s32[]{:S(2)}) async-start(), calls=%async_computation.4 | async-start | bytes 4456448 | tf_op jit(solution)/shard_map/all_gather | solution.py:152
  11.0 140.6 %reduce-scatter.4.cloned.1.call-start = ((), (), s32[]{:S(2)}) async-start(), calls=%async_computation.5 | async-start | bytes 786432 | tf_op jit(solution)/shard_map/reduce_scatter | solution.py:174
  119.5 3.0 copy-start.2
  127.6 5.3 %copy-start.8 = (bf16[1024,16]{0,1:T(8,128)(2,1)S(1)}, bf16[1024,16]{0,1:T(8,128)(2,1)}, u32[]{:S(2)}) copy-start(bf16[1024,16]{0,1:T(8,128)(2,1)} %param.30) | copy-start | bytes 98308
  127.6 10.5 %copy-start.18 = (s32[128]{0:T(128)S(1)}, s32[128]{0:T(128)}, u32[]{:S(2)}) copy-start(s32[128]{0:T(128)} %param.27) | copy-start | bytes 1540
  127.6 10.5 %copy-start.20 = (f32[8,16]{1,0:T(8,128)S(1)}, f32[8,16]{1,0:T(8,128)}, u32[]{:S(2)}) copy-start(f32[8,16]{1,0:T(8,128)} %param.32) | copy-start | bytes 1540
  127.7 23.9 %copy-start.4 = (bf16[128,1024]{1,0:T(8,128)(2,1)S(1)}, bf16[128,1024]{1,0:T(8,128)(2,1)}, u32[]{:S(2)}) copy-start(bf16[128,1024]{1,0:T(8,128)(2,1)} %param.28) | copy-start | bytes 786436
  127.7 23.9 %copy-start.5 = (bf16[16,1024]{1,0:T(8,128)(2,1)S(1)}, bf16[16,1024]{1,0:T(8,128)(2,1)}, u32[]{:S(2)}) copy-start(bf16[16,1024]{1,0:T(8,128)(2,1)} %param.31) | copy-start | bytes 98308
  127.9 26.5 %copy-start.13 = (bf16[8,512]{1,0:T(8,128)(2,1)S(1)}, bf16[8,512]{1,0:T(8,128)(2,1)}, u32[]{:S(2)}) copy-start(bf16[8,512]{1,0:T(8,128)(2,1)} %param.36) | copy-start | bytes 24580
  128.0 26.7 %copy-start.21 = (f32[8,16]{1,0:T(8,128)S(1)}, f32[8,16]{1,0:T(8,128)}, u32[]{:S(2)}) copy-start(f32[8,16]{1,0:T(8,128)} %param.42) | copy-start | bytes 1540
  131.7 42.6 %all-gather.10.cloned.1.call-start = ((), (), s32[]{:S(2)}) async-start(), calls=%async_computation.7 | async-start | bytes 1572864 | tf_op jit(solution)/shard_map/all_gather | solution.py:202
  132.3 81.9 %all-gather.12.cloned.1.call-start = ((), (), s32[]{:S(2)}) async-start(), calls=%async_computation.8 | async-start | bytes 1114112 | tf_op jit(solution)/shard_map/all_gather | solution.py:186
  132.9 103.9 %all-reduce.5.cloned.1.call-start = ((), (), s32[]{:S(2)}) async-start(), calls=%async_computation.6 | async-start | bytes 262144 | tf_op jit(solution)/shard_map/psum | solution.py:189
  138.1 80.8 %copy-start.15 = (f32[128,16]{0,1:T(8,128)}, f32[128,16]{0,1:T(8,128)S(1)}, u32[]{:S(2)}) copy-start(f32[128,16]{0,1:T(8,128)S(1)} %psum.63) | copy-start | bytes 24580
  139.0 15.6 %copy-start.10 = (bf16[128,16]{0,1:T(8,128)(2,1)}, bf16[128,16]{0,1:T(8,128)(2,1)S(1)}, u32[]{:S(2)}) copy-start(bf16[128,16]{0,1:T(8,128)(2,1)S(1)} %get-tuple-element.359) | copy-start | bytes 12292
  153.7 123.2 %all-gather.14.cloned.1.call-start = ((), (), s32[]{:S(2)}) async-start(), calls=%async_computation.9 | async-start | bytes 1114112 | tf_op jit(solution)/shard_map/all_gather | solution.py:185
  154.4 140.0 %reduce-scatter.8.cloned.1.call-start = ((), (), s32[]{:S(2)}) async-start(), calls=%async_computation.11 | async-start | bytes 49152 | tf_op jit(solution)/shard_map/reduce_scatter | solution.py:219
  154.7 64.2 %copy-start.12 = (s32[1024]{0:T(1024)}, s32[1024]{0:T(1024)S(1)}, u32[]{:S(2)}) copy-start(s32[1024]{0:T(1024)S(1)} %eq.32) | copy-start | bytes 12292
  155.2 84.8 %copy-start.17 = (f32[512]{0:T(512)S(1)}, f32[512]{0:T(512)}, u32[]{:S(2)}) copy-start(f32[512]{0:T(512)} %param.37) | copy-start | bytes 6148
  218.9 22.3 %copy-start.6 = (bf16[512,16]{0,1:T(8,128)(2,1)S(1)}, bf16[512,16]{0,1:T(8,128)(2,1)}, u32[]{:S(2)}) copy-start(bf16[512,16]{0,1:T(8,128)(2,1)} %param.40) | copy-start | bytes 49156
  239.4 0.6 copy-start.9
  240.2 1.0 copy-start.3
  276.8 3.0 copy-start.7
  276.8 3.0 copy-start.22
  282.1 1.3 copy-start.1
  284.7 52.9 %reduce-scatter.6.cloned.1.call-start = ((), (), s32[]{:S(2)}) async-start(), calls=%async_computation.10 | async-start | bytes 1572864 | tf_op jit(solution)/shard_map/reduce_scatter | solution.py:213
  289.1 156.2 %all-reduce.7.cloned.1.call-start = ((), (), s32[]{:S(2)}) async-start(), calls=%async_computation.12 | async-start | bytes 393216 | tf_op jit(solution)/shard_map/psum | solution.py:244
  337.6 9.0 %copy-start.11 = (bf16[128,16]{0,1:T(8,128)(2,1)S(1)}, bf16[128,16]{0,1:T(8,128)(2,1)}, u32[]{:S(2)}) copy-start(bf16[128,16]{0,1:T(8,128)(2,1)} %copy-done.10) | copy-start | bytes 12292
  337.6 14.8 %copy-start.14 = (f32[128,16]{0,1:T(8,128)S(1)}, f32[128,16]{0,1:T(8,128)}, u32[]{:S(2)}) copy-start(f32[128,16]{0,1:T(8,128)} %get-tuple-element.360) | copy-start | bytes 24580
  337.6 15.7 %copy-start.16 = (f32[128,16]{0,1:T(8,128)S(1)}, f32[128,16]{0,1:T(8,128)}, u32[]{:S(2)}) copy-start(f32[128,16]{0,1:T(8,128)} %copy-done.15) | copy-start | bytes 24580
  337.6 15.7 %copy-start.19 = (s32[128]{0:T(128)S(1)}, s32[128]{0:T(128)}, u32[]{:S(2)}) copy-start(s32[128]{0:T(128)} %param.27) | copy-start | bytes 1540
Sparse Core Ops, SparseCore 0:
  10.1 55.1 all-gather.5
  67.5 50.6 all-gather.7
  131.9 19.6 reduce-scatter.3
  153.0 21.2 all-gather.9
  176.3 37.8 all-gather.11
  216.3 20.4 all-reduce.4
  239.0 37.8 all-gather.13
  284.8 8.9 reduce-scatter.7
  296.1 20.9 reduce-scatter.5
  353.4 91.8 all-reduce.6
where the time goes:
time: 457 us
  waiting for transfers between devices  295 us (65%)
  blocking collectives  85.4 us (19%)
  matrix products  37.7 us (8%)
  local copies, waits for them, and re-layouts  17.9 us (4%)
  between operations  14.5 us (3%)
    psum x1, waiting for transfers between devices, body(): lax.psum((grad_global_down, grad_global_up, grad_global_scales, grad_loca...  61.7 us
    all_gather x1, waiting for transfers between devices, body(): key_piece = lax.all_gather(patch_keys, 'seq', axis=0, tiled=True)  54.3 us
    all_gather x1, waiting for transfers between devices, body(): value_piece = lax.all_gather(patch_values, 'seq', axis=0, tiled=True)  52.8 us
    psum x1, blocking collectives, body(): lax.psum((grad_local_down, grad_local_scales), ('seq', 'row'))  40.2 us
    all_gather x1, waiting for transfers between devices, body(): lax.all_gather(hidden_out, 'seq', axis=1, tiled=True)  39.9 us
    all_gather x1, waiting for transfers between devices, body(): lax.all_gather(hidden_in, 'seq', axis=1, tiled=True)  34.6 us
    psum x1, blocking collectives, body(): lax.psum((grad_global_down, grad_global_up, grad_global_scales, grad_loca...  30.1 us
    dot_general x12, matrix products, contract(): lax.dot_general(left, right, (((left_dim,), (right_dim,)), ((), ())), pre...  22.4 us
  transfers between devices with their start and end apart: 10, of which 8 were waited for; matrix products, arithmetic and copies ran while one was open for 6% of the time, Pallas kernels for 0%

commit v1 on v0

--- a/solution.py
+++ b/solution.py
@@ -1,8 +1,11 @@
+import functools
 import math
 
 import jax
 import jax.numpy as jnp
 from jax import lax
+from jax.experimental import pallas as pl
+from jax.experimental.pallas import tpu as pltpu
 from jax.sharding import PartitionSpec as P
 
 HEAD = 128
@@ -95,7 +98,7 @@
     return result.reshape(result.shape[0], -1).astype(jnp.bfloat16)
 
 
-def body(
+def general_body(
     patch_queries,
     patch_keys,
     patch_values,
@@ -257,6 +260,491 @@
     )
 
 
+MESH = pl.DeviceIdType.MESH
+
+
+def remote(src, dst, send, recv, seq, row):
+    return pltpu.make_async_remote_copy(
+        src_ref=src,
+        dst_ref=dst,
+        send_sem=send,
+        recv_sem=recv,
+        device_id=(seq, row),
+        device_id_type=MESH,
+    )
+
+
+def greet(peers):
+    barrier = pltpu.get_barrier_semaphore()
+    for seq, row in peers:
+        pl.semaphore_signal(barrier, inc=1, device_id=(seq, row), device_id_type=MESH)
+    pl.semaphore_wait(barrier, len(peers))
+
+
+def front_kernel(
+    chips, depth, q_ref, k_ref, v_ref, w_ref, cot_ref, ow_ref, lw_ref, gd_ref, gu_ref, res_ref,
+    att_out, proj_out, m_out, w_out, cot_out,
+    qb, kb, vb, ob, att, wb, cotb, lwb, w2, acc, e1, e1r, mb, mr,
+    a_send, a_recv, f_send, f_recv, o_send, o_recv, z_send, z_recv, x_send, x_recv,
+    p_send, p_recv, c_send, c_recv, y_send, y_recv,
+):
+    me = lax.axis_index("seq")
+    row = lax.axis_index("row")
+    other = 1 - row
+    chip, core = me // 2, lax.rem(me, 2)
+    mate = 2 * chip + (1 - core)
+    rows = q_ref.shape[0]
+    half = lw_ref.shape[0] // 2
+
+    def at(number):
+        return lax.rem(number + 2 * chips, chips)
+
+    def heads_of(number):
+        return pl.ds(pl.multiple_of(number * HEAD, HEAD), HEAD)
+
+    greet([(2 * at(chip + d) + core, row) for d in range(1, chips)] + [(mate, row), (me, other)])
+
+    own = heads_of(chip)
+    sends = []
+    arrivals = {}
+    own_half = pl.ds(pl.multiple_of(core * half, half), half)
+    mate_half = pl.ds(pl.multiple_of((1 - core) * half, half), half)
+    lw_copy = remote(lw_ref.at[own_half], lwb.at[own_half], y_send.at[0], y_recv.at[0], me, other)
+    lw_copy.start()
+    forwards = {}
+    order = sorted(range(1, chips), key=lambda d: -min(d, chips - d))
+    for d in order:
+        to = at(chip + d)
+        for which, (src, dst) in enumerate(
+            ((k_ref, kb.at[me]), (v_ref, vb.at[me]), (q_ref, qb.at[chip]))
+        ):
+            copy = remote(
+                src.at[:, heads_of(to)], dst, a_send.at[which, d], a_recv.at[which, d],
+                2 * to + core, row,
+            )
+            copy.start()
+            arrivals[which, d] = copy
+    for which, (src, dst) in enumerate(((k_ref, kb), (v_ref, vb))):
+        copy = remote(
+            src.at[:, own], dst.at[me], f_send.at[which, 0], f_recv.at[which, 0], mate, row
+        )
+        copy.start()
+        forwards[which, 0] = copy
+    cot_copy = remote(cot_ref, cotb, c_send.at[0], c_recv.at[0], me, other)
+    cot_copy.start()
+
+    levels = chips // depth
+    level, side = chip // depth, lax.rem(chip, depth)
+    z_copies = []
+    for d in range(1, levels):
+        to = lax.rem(level + d, levels) * depth + side
+        copy = remote(w_ref, wb.at[me], z_send.at[d], z_recv.at[d], 2 * to + core, row)
+        copy.start()
+        z_copies.append((d, copy))
+    neighbour = 2 * (level * depth + (1 - side)) + core
+    x_copies = []
+    p_copies = []
+
+    def pass_side(d, src, slot):
+        copy = remote(src, wb.at[slot], x_send.at[d], x_recv.at[d], neighbour, row)
+        copy.start()
+        x_copies.append((d, copy))
+
+    def pass_mate(number, src, slot):
+        copy = remote(src, wb.at[slot], p_send.at[number], p_recv.at[number], mate, row)
+        copy.start()
+        p_copies.append(copy)
+
+    pass_side(0, w_ref, me)
+    pass_mate(0, w_ref, me)
+
+    qb[chip] = q_ref[:, own]
+    kb[me] = k_ref[:, own]
+    vb[me] = v_ref[:, own]
+    wb[me] = w_ref[...]
+
+    mb[...] = jnp.dot(
+        gu_ref[...], lw_ref[...], preferred_element_type=jnp.float32
+    ).astype(jnp.bfloat16)
+    m_copy = remote(mb, mr, y_send.at[2], y_recv.at[2], me, other)
+    m_copy.start()
+
+    width = lw_ref.shape[0]
+    tile = math.gcd(ow_ref.shape[0], 256)
+    columns = lw_ref.shape[1]
+
+    @pl.loop(0, ow_ref.shape[0] // tile)
+    def _(index):
+        part = pl.ds(pl.multiple_of(index * tile, tile), tile)
+        acc[part] = jnp.dot(
+            ow_ref[part, pl.ds(pl.multiple_of(row * width, width), width)],
+            lw_ref[...],
+            preferred_element_type=jnp.float32,
+        )
+
+    lw_copy.wait_recv()
+    lw_mate = remote(lwb.at[own_half], lwb.at[own_half], y_send.at[1], y_recv.at[1], mate, row)
+    lw_mate.start()
+    lw_mate.wait_recv()
+
+    @pl.loop(0, ow_ref.shape[0] // tile)
+    def _(index):
+        part = pl.ds(pl.multiple_of(index * tile, tile), tile)
+        total = acc[part] + jnp.dot(
+            ow_ref[part, pl.ds(pl.multiple_of(other * width, width), width)],
+            lwb[...],
+            preferred_element_type=jnp.float32,
+        )
+        w2[part, :columns] = total.astype(jnp.bfloat16)
+        w2[part, columns:] = gd_ref[part]
+
+    for d in reversed(range(1, chips)):
+        for which, buffer in ((0, kb), (1, vb)):
+            arrivals[which, d].wait_recv()
+            slot = 2 * at(chip - d) + core
+            copy = remote(
+                buffer.at[slot], buffer.at[slot], f_send.at[which, d], f_recv.at[which, d],
+                mate, row,
+            )
+            copy.start()
+            forwards[which, d] = copy
+        arrivals[2, d].wait_recv()
+    for copy in forwards.values():
+        copy.wait_recv()
+
+    scale = 1.0 / math.sqrt(HEAD)
+    for i in reversed(range(chips)):
+        span = (2 * i + 2) * rows
+        keys = kb[: 2 * i + 2].reshape(span, HEAD)
+        values = vb[: 2 * i + 2].reshape(span, HEAD)
+        scores = contract(qb[i], keys, 1, 1) * scale
+        last = 2 * rows
+        places = lax.broadcasted_iota(jnp.int32, (rows, span), 1)
+        queries = lax.broadcasted_iota(jnp.int32, (rows, span), 0) + (2 * i + core) * rows
+        scores = jnp.where(places <= queries, scores, -1e30)
+        top = jnp.max(scores, axis=1, keepdims=True)
+        weights = jnp.exp(scores - top)
+        mass = jnp.sum(weights, axis=1, keepdims=True)
+        mixed = jnp.dot(weights.astype(jnp.bfloat16), values, preferred_element_type=jnp.float32)
+        ob[i] = (mixed / mass).astype(jnp.bfloat16)
+
+        @pl.when(i != chip)
+        def _():
+            remote(
+                ob.at[i], att.at[:, own], o_send.at[i], o_recv.at[chip], 2 * i + core, row
+            ).start()
+
+        @pl.when(i == chip)
+        def _():
+            att[:, own] = ob[i]
+
+    for d, copy in z_copies:
+        copy.wait_recv()
+        slot = 2 * (lax.rem(level - d + levels, levels) * depth + side) + core
+        pass_side(d, wb.at[slot], slot)
+        pass_mate(d, wb.at[slot], slot)
+    for d, copy in list(x_copies):
+        copy.wait_recv()
+        slot = 2 * (lax.rem(level - d + levels, levels) * depth + (1 - side)) + core
+        pass_mate(levels + d, wb.at[slot], slot)
+
+    for i in range(chips):
+
+        @pl.when(i != chip)
+        def _():
+            back = remote(
+                ob.at[i], att.at[:, heads_of(i)], o_send.at[i], o_recv.at[i], 2 * i + core, row
+            )
+            back.wait_recv()
+            back.wait_send()
+
+    value = jnp.dot(att[...], w2[...], preferred_element_type=jnp.float32)
+    e1[:, :columns] = (
+        value[:, :columns]
+        + jnp.dot(res_ref[...], lw_ref[...], preferred_element_type=jnp.float32)
+    ).astype(jnp.bfloat16)
+    e1[:, columns:] = value[:, columns:].astype(jnp.bfloat16)
+    e_copy = remote(e1, e1r, y_send.at[3], y_recv.at[3], me, other)
+    e_copy.start()
+    att_out[...] = att[...]
+    cot_copy.wait_recv()
+    cot_out[row] = cot_ref[...]
+    cot_out[other] = cotb[...]
+    m_copy.wait_recv()
+    m_out[...] = mb[...].astype(jnp.float32) + mr[...].astype(jnp.float32)
+    for copy in p_copies:
+        copy.wait_recv()
+    shard = w_ref.shape[0] // 2
+    w_out[0] = wb[:, :shard]
+    w_out[1] = wb[:, shard:]
+    e_copy.wait_recv()
+    proj_out[...] = e1[...].astype(jnp.float32) + e1r[...].astype(jnp.float32)
+    for copy in (
+        [lw_copy, lw_mate, cot_copy, m_copy, e_copy]
+        + list(arrivals.values())
+        + list(forwards.values())
+        + [copy for d, copy in z_copies + x_copies]
+        + p_copies
+    ):
+        copy.wait_send()
+
+
+def front(q, k, v, w, cot, ow, lw, gd, gu, res, count):
+    chips = q.shape[1] // HEAD
+    rows = q.shape[0]
+    depth = 2
+    levels = chips // depth
+    columns = lw.shape[1]
+    wide = columns + gd.shape[1]
+    vm = pl.BlockSpec(memory_space=pltpu.VMEM)
+    dma = pltpu.SemaphoreType.DMA
+    bf, f32 = jnp.bfloat16, jnp.float32
+    return pl.pallas_call(
+        functools.partial(front_kernel, chips, depth),
+        out_shape=(
+            jax.ShapeDtypeStruct(q.shape, bf),
+            jax.ShapeDtypeStruct((rows, wide), f32),
+            jax.ShapeDtypeStruct((gu.shape[0], columns), f32),
+            jax.ShapeDtypeStruct((2, count, w.shape[0] // 2, w.shape[1]), bf),
+            jax.ShapeDtypeStruct((2,) + cot.shape, bf),
+        ),
+        in_specs=[vm] * 10,
+        out_specs=(vm,) * 5,
+        scratch_shapes=[
+            pltpu.VMEM((chips, rows, HEAD), bf),
+            pltpu.VMEM((count, rows, HEAD), bf),
+            pltpu.VMEM((count, rows, HEAD), bf),
+            pltpu.VMEM((chips, rows, HEAD), bf),
+            pltpu.VMEM(q.shape, bf),
+            pltpu.VMEM((count,) + w.shape, bf),
+            pltpu.VMEM(cot.shape, bf),
+            pltpu.VMEM(lw.shape, bf),
+            pltpu.VMEM((ow.shape[0], wide), bf),
+            pltpu.VMEM((ow.shape[0], columns), f32),
+            pltpu.VMEM((rows, wide), bf),
+            pltpu.VMEM((rows, wide), bf),
+            pltpu.VMEM((gu.shape[0], columns), bf),
+            pltpu.VMEM((gu.shape[0], columns), bf),
+            dma((3, chips)), dma((3, chips)),
+            dma((2, chips)), dma((2, chips)),
+            dma((chips,)), dma((chips,)),
+            dma((levels,)), dma((levels,)),
+            dma((levels,)), dma((levels,)),
+            dma((chips,)), dma((chips,)),
+            dma((1,)), dma((1,)),
+            dma((4,)), dma((4,)),
+        ],
+        compiler_params=pltpu.CompilerParams(
+            collective_id=0, has_side_effects=True, vmem_limit_bytes=60 * 1024 * 1024
+        ),
+        name="front",
+    )(q, k, v, w, cot, ow, lw, gd, gu, res)
+
+
+def swap_kernel(x_ref, o_ref, buf, send, recv):
+    me, row = lax.axis_index("seq"), lax.axis_index("row")
+    greet([(me, 1 - row)])
+    copy = remote(x_ref, buf, send, recv, me, 1 - row)
+    copy.start()
+    copy.wait()
+    o_ref[...] = x_ref[...].astype(jnp.float32) + buf[...].astype(jnp.float32)
+
+
+def row_sum(x):
+    vm = pl.BlockSpec(memory_space=pltpu.VMEM)
+    return pl.pallas_call(
+        swap_kernel,
+        out_shape=jax.ShapeDtypeStruct(x.shape, jnp.float32),
+        in_specs=[vm],
+        out_specs=vm,
+        scratch_shapes=[
+            pltpu.VMEM(x.shape, x.dtype), pltpu.SemaphoreType.DMA, pltpu.SemaphoreType.DMA
+        ],
+        compiler_params=pltpu.CompilerParams(collective_id=1, has_side_effects=True),
+        name="row_sum",
+    )(x)
+
+
+def total_kernel(count, shared, g_ref, o_ref, part, result, full, s1, r1, s2, r2, s3, r3):
+    me, row = lax.axis_index("seq"), lax.axis_index("row")
+    other = 1 - row
+    peers = [(lax.rem(me + d, count), row) for d in range(1, count)]
+    cross = [(lax.rem(me + d, count), other) for d in range(count)]
+    greet(peers + cross)
+    first = []
+    for d in range(1, count):
+        to = lax.rem(me + d, count)
+        copy = remote(g_ref.at[to], part.at[row, me], s1.at[d], r1.at[d], to, row)
+        copy.start()
+        first.append(copy)
+    crossing = []
+    for index, to in enumerate(shared):
+        copy = remote(g_ref.at[to], part.at[row, me], s3.at[index], r3.at[me], to, other)
+        copy.start()
+        crossing.append(copy)
+    part[row, me] = g_ref[me]
+    for copy in first:
+        copy.wait_recv()
+
+    def add(side):
+        return jnp.sum(part[side].astype(jnp.float32), axis=0)
+
+    result[...] = add(row).astype(jnp.bfloat16)
+
+    @pl.when(me >= shared[0])
+    def _():
+        for source in range(count):
+            remote(
+                g_ref.at[0], part.at[other, source], s3.at[0], r3.at[source], me, other
+            ).wait_recv()
+        result[...] = (add(0) + add(1)).astype(jnp.bfloat16)
+
+    second = []
+    for d in range(1, count):
+        to = lax.rem(me + d, count)
+        copy = remote(result, full.at[me], s2.at[d], r2.at[d], to, row)
+        copy.start()
+        second.append(copy)
+    full[me] = result[...]
+    for copy in second:
+        copy.wait_recv()
+    o_ref[...] = full[...].astype(jnp.float32)
+    for copy in first + crossing + second:
+        copy.wait_send()
+
+
+def grand_total(g, shared):
+    count = g.shape[0]
+    vm = pl.BlockSpec(memory_space=pltpu.VMEM)
+    dma = pltpu.SemaphoreType.DMA
+    return pl.pallas_call(
+        functools.partial(total_kernel, count, shared),
+        out_shape=jax.ShapeDtypeStruct(g.shape, jnp.float32),
+        in_specs=[vm],
+        out_specs=vm,
+        scratch_shapes=[
+            pltpu.VMEM((2,) + g.shape, g.dtype),
+            pltpu.VMEM(g.shape[1:], g.dtype),
+            pltpu.VMEM(g.shape, g.dtype),
+            dma((count,)), dma((count,)),
+            dma((count,)), dma((count,)),
+            dma((len(shared),)), dma((count,)),
+        ],
+        compiler_params=pltpu.CompilerParams(collective_id=2, has_side_effects=True),
+        name="grand_total",
+    )(g)
+
+
+def paired_body(
+    patch_queries,
+    patch_keys,
+    patch_values,
+    patch_tasks,
+    residual,
+    output_weight,
+    global_down,
+    global_up,
+    global_scales,
+    local_weight,
+    byte_ids,
+    byte_table,
+    position_table,
+    norm_gain,
+    hidden_in,
+    hidden_out,
+    local_down,
+    local_up,
+    local_scales,
+    cotangent,
+):
+    count = lax.axis_size("seq")
+    bf = jnp.bfloat16
+    rank = global_up.shape[0]
+    columns = local_weight.shape[1]
+    hidden = hidden_in.shape[0]
+    shards = jnp.concatenate([jnp.transpose(hidden_in), jnp.transpose(hidden_out)], axis=0)
+    wide_down = jnp.pad(global_down, ((0, 0), (0, HEAD - rank)))
+    attended, proj, bridge, weights, cot = front(
+        patch_queries, patch_keys, patch_values, shards, cotangent, output_weight,
+        local_weight, wide_down, global_up, residual, count,
+    )
+    reduced = proj[:, columns : columns + rank]
+    rows_in = weights[0].reshape(columns, hidden)
+    rows_out = weights[1].reshape(columns, hidden)
+    cot = cot.reshape(-1, columns)
+    task_scales = select_rows(global_scales, patch_tasks)
+    scaled = (reduced * task_scales).astype(bf)
+    bridge_b = bridge.astype(bf)
+    projected = (
+        proj[:, :columns] + jnp.dot(scaled, bridge_b, preferred_element_type=jnp.float32)
+    ).astype(bf)
+    inputs, inverse, normed, lowered, scales, shrunk, byte_tasks = local_inputs(
+        byte_ids, projected, patch_tasks, byte_table, position_table, norm_gain, local_down,
+        local_scales,
+    )
+    upper = jnp.dot(normed, rows_in, preferred_element_type=jnp.float32) + jnp.dot(
+        shrunk, local_up, preferred_element_type=jnp.float32
+    )
+    through = jnp.dot(cot, rows_out, preferred_element_type=jnp.float32)
+    grown = (through * gelu_slope(upper)).astype(bf)
+    grad_local_up = contract(shrunk, grown, 0, 0)
+    back_rank = contract(grown, local_up, 1, 1)
+    moved = (back_rank * scales).astype(bf)
+    grad_local_scales = task_totals(byte_tasks, back_rank * lowered)
+    grad_local_down = contract(moved, normed, 0, 0)
+    back_total = contract(grown, rows_in, 1, 1) + contract(moved, local_down, 1, 1)
+    gained = back_total * norm_gain
+    average = jnp.mean(gained * inputs, axis=1, keepdims=True)
+    back_inputs = inverse * (gained - inputs * inverse * inverse * average)
+    patches = patch_tasks.shape[0]
+    back_part = back_inputs.reshape(patches, PATCH, -1).sum(axis=1).astype(bf)
+    cot_sum = cot.astype(jnp.float32).reshape(patches, PATCH, -1).sum(axis=1)
+    patch_grad = (row_sum(back_part) + cot_sum).astype(bf)
+    back_mixed = contract(patch_grad, local_weight, 1, 1).astype(bf)
+    grad_global_up = contract(scaled, back_mixed, 0, 0)
+    back_scaled = contract(patch_grad, bridge_b, 1, 1)
+    grad_global_scales = task_totals(patch_tasks, back_scaled * reduced)
+    back_reduced = (back_scaled * task_scales).astype(bf)
+    grad_global_down = contract(back_reduced, attended, 0, 0)
+
+    spare = hidden - columns - rank
+    small = jnp.concatenate([0.5 * grad_global_scales, grad_local_scales], axis=0)
+    last = jnp.concatenate(
+        [grad_local_down, small, jnp.zeros((rank, spare), jnp.float32)], axis=1
+    )
+    packed = jnp.concatenate(
+        [grad_global_down, grad_global_up, grad_local_up, last], axis=0
+    ).astype(bf)
+    blocks = packed.reshape(count, 16, -1)
+    shared = tuple(range(count - count // 4, count))
+    summed = grand_total(blocks, shared).reshape(packed.shape)
+    last = summed[3 * rank :]
+    return (
+        jnp.transpose(summed[:rank]),
+        summed[rank : 2 * rank],
+        last[:TASKS, columns : columns + rank],
+        jnp.transpose(last[:, :columns]),
+        summed[2 * rank : 3 * rank],
+        last[TASKS:, columns : columns + rank],
+    )
+
+
+def pick_body(seq_count, row_count, *args):
+    heads = args[0].shape[1] // HEAD
+    rank = args[7].shape[0]
+    hidden = args[14].shape[0]
+    fits = (
+        row_count == 2
+        and seq_count == 2 * heads
+        and heads % 4 == 0
+        and rank == 2 * TASKS
+        and args[0].shape[1] == hidden
+        and (4 * rank * hidden) % (seq_count * 16 * HEAD) == 0
+        and hidden >= args[9].shape[1] + rank
+    )
+    return paired_body(*args) if fits else general_body(*args)
+
+
 def solution(mesh):
     placed = (
         P("seq", "row"),
@@ -280,8 +768,9 @@
         P(),
         P(("seq", "row"), None),
     )
+    chosen = functools.partial(pick_body, mesh.shape["seq"], mesh.shape["row"])
     return jax.shard_map(
-        body,
+        chosen,
         mesh=mesh,
         in_specs=placed,
         out_specs=(P("row", None), P(None, "row"), P(), P(), P(None, "row"), P()),

time: 457 us -> 116 us (0.25)
  waiting for transfers between devices: 295 us -> 0 us
  blocking collectives: 85.4 us -> 0 us
  Pallas kernels: 0 us -> 84.6 us
  matrix products: 37.7 us -> 13 us
  between operations: 14.5 us -> 0.9 us
  local copies, waits for them, and re-layouts: 17.9 us -> 9.93 us
    all_gather x5 -> x0, waiting for transfers between devices: 201 us -> none  [the longest x1 54.3 us: body(): key_piece = lax.all_gather(patch_keys, 'seq', axis=0, tiled=True)]
    pallas_call x0 -> x3, Pallas kernels: none -> 84.6 us  [the longest x1 55.1 us: front(): pl.pallas_call(functools.partial(front_kernel, chips, depth), out_shape=(...]
    psum x4 -> x0, blocking collectives: 80.2 us -> none  [the longest x1 40.2 us: body(): lax.psum((grad_local_down, grad_local_scales), ('seq', 'row'))]
    psum x2 -> x0, waiting for transfers between devices: 79.6 us -> none  [the longest x1 61.7 us: body(): lax.psum((grad_global_down, grad_global_up, grad_global_scales, grad_loca...]
    dot_general x12 -> x8, matrix products: 22.4 us -> 4.11 us  [contract(): lax.dot_general(left, right, (((left_dim,), (right_dim,)), ((), ())), pre...]
    reduce_scatter x3 -> x0, waiting for transfers between devices: 12.6 us -> none  [the longest x1 12.6 us: body(): lax.psum_scatter(contract(output_weight, attended, 0, 1).astype(jnp.bfloa...]
    unnamed x49 -> x23, local copies, waits for them, and re-layouts: 11.1 us -> 1.42 us
    all_gather x1 -> x0, blocking collectives: 5.17 us -> none  [body(): lax.all_gather(patch_grad, 'row', axis=0, tiled=True)]
  transfers between devices with their start and end apart: 10 -> 0, of which waited for: 8 -> 0; matrix products, arithmetic and copies ran while one was open for 6% -> 0% of each run, Pallas kernels for 0% -> 0%
where the time goes in v1:
time: 116 us; the launch traced here: 115 us
  Pallas kernels  84.6 us (73%)
  matrix products  13 us (11%)
  local copies, waits for them, and re-layouts  9.93 us (9%)
  other arithmetic  6.75 us (6%)
    pallas_call x1, Pallas kernels, front(): pl.pallas_call(functools.partial(front_kernel, chips, depth), out_shape=(...  55.1 us
    pallas_call x1, Pallas kernels, grand_total(): pl.pallas_call(functools.partial(total_kernel, count, shared), out_shape=...  22.9 us
    pallas_call x1, Pallas kernels, row_sum(): pl.pallas_call(swap_kernel, out_shape=jax.ShapeDtypeStruct(x.shape, jnp.f...  6.63 us
    dot_general x8, matrix products, contract(): lax.dot_general(left, right, (((left_dim,), (right_dim,)), ((), ())), pre...  4.11 us

profile of v1, /device:TPU:0, one launch (start us, length us, event | category | flops | bytes accessed | tf_op | source)
XLA Modules:
  0.0 115.2 jit_solution(16671274007513137373)
XLA Ops:
  0.6 0.0 copy-start
  0.6 0.9 fusion.19
  1.6 0.8 convert_element_type.58
  2.4 0.1 copy.30
  2.5 0.7 eq.23
  3.2 0.1 eq.26
  3.3 1.2 %fusion.12 = f32[1024,16]{0,1:T(8,128)S(1)} fusion(f32[8,16]{1,0:T(8,128)} %param.38, s32[1024]{0:T(1024)S(1)} %eq.26), kind=kOutput, calls=%fused_computation.30 | convolution fusion | flops 1581056 | bytes 70144 | tf_op jit(solution)/shard_map/dot_general | solution.py:27
  4.4 1.5 %pad_maximum_fusion.w_ref = bf16[64,1024]{1,0:T(8,128)(2,1)} fusion(bf16[32,1024]{1,0:T(8,128)(2,1)} %bitcast.51, bf16[32,1024]{1,0:T(8,128)(2,1)} %bitcast.52), kind=kLoop, calls=%fused_computation.35 | loop fusion | flops 262144 | bytes 262144 | tf_op jit(solution)/shard_map/concatenate | solution.py:665
  6.0 0.9 copy.29
  6.9 0.8 pad.4.gd_ref
  7.7 55.1 %front.1 = (bf16[128,1024]{1,0:T(8,128)(2,1)}, f32[128,640]{1,0:T(8,128)}, f32[16,512]{1,0:T(8,128)}, bf16[2,16,32,1024]{3,2,1,0:T(8,128)(2,1)}, bf16[2,512,512]{2,1,0:T(8,128)(2,1)}) custom-call(bf16[128,1024]{1,0:T(8,128)(2,1)} %q_ref.1, bf16[128,1024]{1,0:T(8,128)(2,1)} %k_ref.1, bf16[128,1024]{1,0:T(8,128)(2,1)} %v_ref.1, ...), custom_call_target="tpu_custom_call" | custom-call | tf_op jit(solution)/shard_map/front/pallas_call | solution.py:502
  62.8 0.9 multiply_convert_fusion.3
  63.6 0.0 copy-start.2
  63.6 0.0 copy-start.3
  63.6 0.0 copy-start.5
  63.6 0.0 copy-start.10
  63.7 1.8 %fusion.26 = (bf16[1,16,32,1024]{3,2,1,0:T(8,128)(2,1)S(1)}, bf16[1,16,32,1024]{3,2,1,0:T(8,128)(2,1)S(1)}) fusion(bf16[2,16,32,1024]{3,2,1,0:T(8,128)(2,1)} %get-tuple-element.14), kind=kLoop, calls=%fused_computation.54 | loop fusion | bytes 4194304 | tf_op jit(solution)/shard_map/slice | solution.py:672
  65.5 0.0 copy-done.2
  65.5 0.7 convert_reduce_fusion
  66.2 0.0 copy-done.3
  66.2 0.0 copy-done.5
  66.2 0.0 copy-start.8
  66.2 0.2 fusion.8
  66.4 0.0 copy-done
  66.4 0.0 copy-done.10
  66.4 0.7 multiply_reduce_fusion.1
  67.1 0.0 copy-start.6
  67.1 0.0 copy-done.8
  67.1 0.2 multiply_convert_fusion
  67.4 0.4 copy-done.6
  67.8 0.4 multiply_convert_fusion.2
  68.2 1.3 %fusion.29 = f32[1024,1024]{1,0:T(8,128)S(1)} fusion(bf16[1024,512]{1,0:T(8,128)(2,1)S(1)} %bitcast.46, bf16[512,1024]{1,0:T(8,128)(2,1)S(1)} %bitcast.49), kind=kOutput, calls=%fused_computation.57 | convolution fusion | flops 1073741824 | bytes 6291456 | tf_op jit(solution)/shard_map/dot_general | solution.py:688
  69.5 0.0 copy-start.7
  69.5 1.3 %fusion.30 = f32[1024,1024]{1,0:T(8,128)S(1)} fusion(bf16[1024,512]{1,0:T(8,128)(2,1)S(1)} %multiply_convert_fusion, bf16[512,1024]{1,0:T(8,128)(2,1)S(1)} %bitcast.47), kind=kOutput, calls=%fused_computation.58 | convolution fusion | flops 1073741824 | bytes 6291456 | tf_op jit(solution)/shard_map/dot_general | solution.py:685
  70.7 0.0 copy-done.7
  70.8 2.3 %fusion.5 = bf16[1024,1024]{1,0:T(8,128)(2,1)S(1)} fusion(f32[1024,1024]{1,0:T(8,128)S(1)} %fusion.29, f32[1024,1024]{1,0:T(8,128)S(1)} %fusion.30, bf16[1024,16]{0,1:T(8,128)(2,1)S(1)} %get-tuple-element.26, bf16[16,1024]{1,0:T(8,128)(2,1)S(1)} %copy-done.7), kind=kOutput, calls=%fused_computation.6 | convolution fusion | flops 45088768 | bytes 10551296 | tf_op jit(solution)/shard_map/dot_general | solution.py:685
  73.0 0.4 convolution_convert_fusion.1
  73.4 0.7 multiply_convert_fusion.1
  74.1 1.3 %fusion.31 = f32[1024,512]{1,0:T(8,128)S(1)} fusion(bf16[1024,1024]{1,0:T(8,128)(2,1)S(1)} %fusion.5, bf16[512,1024]{1,0:T(8,128)(2,1)S(1)} %bitcast.48), kind=kOutput, calls=%fused_computation.59 | convolution fusion | flops 1073741824 | bytes 5242880 | tf_op jit(solution)/shard_map/dot_general | solution.py:18
  75.4 0.2 convolution_convert_fusion.3
  75.6 0.6 convolution_convert_fusion.4
  76.2 0.6 multiply_reduce_fusion
  76.8 0.0 copy-start.4
  76.8 0.0 copy-start.1
  76.8 1.6 %bitcast_reduce_fusion.x_ref = bf16[128,512]{1,0:T(8,128)(2,1)} fusion(f32[1024,512]{1,0:T(8,128)S(1)} %get-tuple-element.31, f32[1024,512]{1,0:T(8,128)S(1)} %get-tuple-element.25, f32[1024]{0:T(1024)S(1)} %broadcast_multiply_fusion, f32[1024]{0:T(1024)S(1)} %add_rsqrt_fusion), kind=kLoop, calls=%fused_computation.8 | loop fusion | flops 3080192 | bytes 4333568 | tf_op jit(solution)/shard_map/reduce_sum | solution.py:700
  78.4 6.6 %row_sum.1 = f32[128,512]{1,0:T(8,128)} custom-call(bf16[128,512]{1,0:T(8,128)(2,1)} %bitcast_reduce_fusion.x_ref), custom_call_target="tpu_custom_call" | custom-call | tf_op jit(solution)/shard_map/row_sum/pallas_call | solution.py:555
  85.0 1.0 add_convert_fusion
  86.0 0.1 fusion.23
  86.2 0.0 copy-done.4
  86.2 0.2 convolution_convert_fusion.2
  86.3 0.0 copy-done.1
  86.3 0.6 fusion.9
  86.9 0.1 copy.31
  87.0 0.0 copy-done.9
  87.1 0.3 fusion.10
  87.3 0.1 maximum_maximum_fusion
  87.4 0.7 convert_element_type.73.g_ref
  88.2 22.9 %grand_total.1 = f32[16,16,256]{2,1,0:T(8,128)} custom-call(bf16[16,16,256]{2,1,0:T(8,128)(2,1)} %convert_element_type.73.g_ref), custom_call_target="tpu_custom_call" | custom-call | tf_op jit(solution)/shard_map/grand_total/pallas_call | solution.py:620
  111.1 1.0 fusion.27
  112.0 0.6 slice.58
  112.7 0.6 fusion.28
  113.3 0.6 slice_bitcast_fusion
  113.9 0.6 slice.52
  114.6 0.6 slice.50
  (5 shorter events, 0.0 us)
Async XLA Ops:
  0.6 65.8 %copy-start = (bf16[256,512]{1,0:T(8,128)(2,1)S(1)}, bf16[256,512]{1,0:T(8,128)(2,1)}, u32[]{:S(2)}) copy-start(bf16[256,512]{1,0:T(8,128)(2,1)} %param.31) | copy-start | bytes 786436
  63.6 1.9 %copy-start.2 = (bf16[2,512,512]{2,1,0:T(8,128)(2,1)S(1)}, bf16[2,512,512]{2,1,0:T(8,128)(2,1)}, u32[]{:S(2)}) copy-start(bf16[2,512,512]{2,1,0:T(8,128)(2,1)} %get-tuple-element.13) | copy-start | bytes 3145732
  63.6 2.6 %copy-start.3 = (f32[128,640]{1,0:T(8,128)S(1)}, f32[128,640]{1,0:T(8,128)}, u32[]{:S(2)}) copy-start(f32[128,640]{1,0:T(8,128)} %get-tuple-element.11) | copy-start | bytes 983044
  63.6 2.6 %copy-start.5 = (f32[16,512]{1,0:T(8,128)S(1)}, f32[16,512]{1,0:T(8,128)}, u32[]{:S(2)}) copy-start(f32[16,512]{1,0:T(8,128)} %get-tuple-element.12) | copy-start | bytes 98308
  63.6 2.8 %copy-start.10 = (s32[1024]{0:T(1024)S(1)}, s32[1024]{0:T(1024)}, u32[]{:S(2)}) copy-start(s32[1024]{0:T(1024)} %param.30) | copy-start | bytes 12292
  66.2 0.9 copy-start.8
  67.1 0.7 copy-start.6
  69.5 1.3 %copy-start.7 = (bf16[16,1024]{1,0:T(8,128)(2,1)S(1)}, bf16[16,1024]{1,0:T(8,128)(2,1)}, u32[]{:S(2)}) copy-start(bf16[16,1024]{1,0:T(8,128)(2,1)} %param.37) | copy-start | bytes 98308
  76.8 9.4 %copy-start.4 = (bf16[128,1024]{1,0:T(8,128)(2,1)S(1)}, bf16[128,1024]{1,0:T(8,128)(2,1)}, u32[]{:S(2)}) copy-start(bf16[128,1024]{1,0:T(8,128)(2,1)} %get-tuple-element.15) | copy-start | bytes 786436
  76.8 9.5 %copy-start.1 = (bf16[1024,512]{1,0:T(8,128)(2,1)S(1)}, bf16[1024,512]{1,0:T(8,128)(2,1)}, u32[]{:S(2)}) copy-start(bf16[1024,512]{1,0:T(8,128)(2,1)} %lw_ref.1) | copy-start | bytes 3145732
  78.4 8.6 %copy-start.9 = (s32[128]{0:T(128)S(1)}, s32[128]{0:T(128)}, u32[]{:S(2)}) copy-start(s32[128]{0:T(128)} %param.23) | copy-start | bytes 1540

commit v2 on v1

--- a/solution.py
+++ b/solution.py
@@ -282,9 +282,9 @@
 
 
 def front_kernel(
-    chips, depth, q_ref, k_ref, v_ref, w_ref, cot_ref, ow_ref, lw_ref, gd_ref, gu_ref, res_ref,
-    att_out, proj_out, m_out, w_out, cot_out,
-    qb, kb, vb, ob, att, wb, cotb, lwb, w2, acc, e1, e1r, mb, mr,
+    chips, depth, q_ref, k_ref, v_ref, hi_ref, ho_ref, cot_ref, ow_hbm, lw_ref, gd_ref, gu_ref,
+    res_ref, att_out, proj_out, m_out, hi_out, ho_out, cot_out,
+    ow_ref, ow_sem, qb, kb, vb, ob, att, wb, cotb, lwb, w2, acc, e1, e1r, mb, mr,
     a_send, a_recv, f_send, f_recv, o_send, o_recv, z_send, z_recv, x_send, x_recv,
     p_send, p_recv, c_send, c_recv, y_send, y_recv,
 ):
@@ -302,6 +302,11 @@
     def heads_of(number):
         return pl.ds(pl.multiple_of(number * HEAD, HEAD), HEAD)
 
+    ow_copy = pltpu.make_async_copy(ow_hbm, ow_ref, ow_sem)
+    ow_copy.start()
+    shard = hi_ref.shape[0]
+    wb[me, :shard] = hi_ref[...]
+    wb[me, shard:] = ho_ref[...]
     greet([(2 * at(chip + d) + core, row) for d in range(1, chips)] + [(mate, row), (me, other)])
 
     own = heads_of(chip)
@@ -338,7 +343,7 @@
     z_copies = []
     for d in range(1, levels):
         to = lax.rem(level + d, levels) * depth + side
-        copy = remote(w_ref, wb.at[me], z_send.at[d], z_recv.at[d], 2 * to + core, row)
+        copy = remote(wb.at[me], wb.at[me], z_send.at[d], z_recv.at[d], 2 * to + core, row)
         copy.start()
         z_copies.append((d, copy))
     neighbour = 2 * (level * depth + (1 - side)) + core
@@ -355,13 +360,12 @@
         copy.start()
         p_copies.append(copy)
 
-    pass_side(0, w_ref, me)
-    pass_mate(0, w_ref, me)
+    pass_side(0, wb.at[me], me)
+    pass_mate(0, wb.at[me], me)
 
     qb[chip] = q_ref[:, own]
     kb[me] = k_ref[:, own]
     vb[me] = v_ref[:, own]
-    wb[me] = w_ref[...]
 
     mb[...] = jnp.dot(
         gu_ref[...], lw_ref[...], preferred_element_type=jnp.float32
@@ -372,6 +376,8 @@
     width = lw_ref.shape[0]
     tile = math.gcd(ow_ref.shape[0], 256)
     columns = lw_ref.shape[1]
+
+    ow_copy.wait()
 
     @pl.loop(0, ow_ref.shape[0] // tile)
     def _(index):
@@ -395,8 +401,7 @@
             lwb[...],
             preferred_element_type=jnp.float32,
         )
-        w2[part, :columns] = total.astype(jnp.bfloat16)
-        w2[part, columns:] = gd_ref[part]
+        w2[part] = total.astype(jnp.bfloat16)
 
     for d in reversed(range(1, chips)):
         for which, buffer in ((0, kb), (1, vb)):
@@ -460,10 +465,13 @@
 
     value = jnp.dot(att[...], w2[...], preferred_element_type=jnp.float32)
     e1[:, :columns] = (
-        value[:, :columns]
+        value
         + jnp.dot(res_ref[...], lw_ref[...], preferred_element_type=jnp.float32)
     ).astype(jnp.bfloat16)
-    e1[:, columns:] = value[:, columns:].astype(jnp.bfloat16)
+    e1[:, columns:] = jnp.zeros((rows, e1.shape[1] - columns), jnp.bfloat16)
+    e1[:, columns : columns + gd_ref.shape[0]] = contract(att[...], gd_ref[...], 1, 1).astype(
+        jnp.bfloat16
+    )
     e_copy = remote(e1, e1r, y_send.at[3], y_recv.at[3], me, other)
     e_copy.start()
     att_out[...] = att[...]
@@ -474,9 +482,8 @@
     m_out[...] = mb[...].astype(jnp.float32) + mr[...].astype(jnp.float32)
     for copy in p_copies:
         copy.wait_recv()
-    shard = w_ref.shape[0] // 2
-    w_out[0] = wb[:, :shard]
-    w_out[1] = wb[:, shard:]
+    hi_out[...] = wb[:, :shard]
+    ho_out[...] = wb[:, shard:]
     e_copy.wait_recv()
     proj_out[...] = e1[...].astype(jnp.float32) + e1r[...].astype(jnp.float32)
     for copy in (
@@ -489,13 +496,13 @@
         copy.wait_send()
 
 
-def front(q, k, v, w, cot, ow, lw, gd, gu, res, count):
+def front(q, k, v, hi, ho, cot, ow, lw, gd, gu, res, count):
     chips = q.shape[1] // HEAD
     rows = q.shape[0]
     depth = 2
     levels = chips // depth
     columns = lw.shape[1]
-    wide = columns + gd.shape[1]
+    wide = columns + HEAD
     vm = pl.BlockSpec(memory_space=pltpu.VMEM)
     dma = pltpu.SemaphoreType.DMA
     bf, f32 = jnp.bfloat16, jnp.float32
@@ -505,21 +512,24 @@
             jax.ShapeDtypeStruct(q.shape, bf),
             jax.ShapeDtypeStruct((rows, wide), f32),
             jax.ShapeDtypeStruct((gu.shape[0], columns), f32),
-            jax.ShapeDtypeStruct((2, count, w.shape[0] // 2, w.shape[1]), bf),
+            jax.ShapeDtypeStruct((count,) + hi.shape, bf),
+            jax.ShapeDtypeStruct((count,) + ho.shape, bf),
             jax.ShapeDtypeStruct((2,) + cot.shape, bf),
         ),
-        in_specs=[vm] * 10,
-        out_specs=(vm,) * 5,
+        in_specs=[vm] * 6 + [pl.BlockSpec(memory_space=pl.ANY)] + [vm] * 4,
+        out_specs=(vm,) * 6,
         scratch_shapes=[
+            pltpu.VMEM(ow.shape, bf),
+            dma,
             pltpu.VMEM((chips, rows, HEAD), bf),
             pltpu.VMEM((count, rows, HEAD), bf),
             pltpu.VMEM((count, rows, HEAD), bf),
             pltpu.VMEM((chips, rows, HEAD), bf),
             pltpu.VMEM(q.shape, bf),
-            pltpu.VMEM((count,) + w.shape, bf),
+            pltpu.VMEM((count, 2 * hi.shape[0], hi.shape[1]), bf),
             pltpu.VMEM(cot.shape, bf),
             pltpu.VMEM(lw.shape, bf),
-            pltpu.VMEM((ow.shape[0], wide), bf),
+            pltpu.VMEM((ow.shape[0], columns), bf),
             pltpu.VMEM((ow.shape[0], columns), f32),
             pltpu.VMEM((rows, wide), bf),
             pltpu.VMEM((rows, wide), bf),
@@ -538,7 +548,7 @@
             collective_id=0, has_side_effects=True, vmem_limit_bytes=60 * 1024 * 1024
         ),
         name="front",
-    )(q, k, v, w, cot, ow, lw, gd, gu, res)
+    )(q, k, v, hi, ho, cot, ow, lw, gd, gu, res)
 
 
 def swap_kernel(x_ref, o_ref, buf, send, recv):
@@ -662,15 +672,14 @@
     rank = global_up.shape[0]
     columns = local_weight.shape[1]
     hidden = hidden_in.shape[0]
-    shards = jnp.concatenate([jnp.transpose(hidden_in), jnp.transpose(hidden_out)], axis=0)
-    wide_down = jnp.pad(global_down, ((0, 0), (0, HEAD - rank)))
-    attended, proj, bridge, weights, cot = front(
-        patch_queries, patch_keys, patch_values, shards, cotangent, output_weight,
-        local_weight, wide_down, global_up, residual, count,
+    attended, proj, bridge, rows_in, rows_out, cot = front(
+        patch_queries, patch_keys, patch_values, jnp.transpose(hidden_in),
+        jnp.transpose(hidden_out), cotangent, output_weight, local_weight,
+        jnp.transpose(global_down), global_up, residual, count,
     )
     reduced = proj[:, columns : columns + rank]
-    rows_in = weights[0].reshape(columns, hidden)
-    rows_out = weights[1].reshape(columns, hidden)
+    rows_in = rows_in.reshape(columns, hidden)
+    rows_out = rows_out.reshape(columns, hidden)
     cot = cot.reshape(-1, columns)
     task_scales = select_rows(global_scales, patch_tasks)
     scaled = (reduced * task_scales).astype(bf)

time: 116 us -> 113 us (0.974)
  local copies, waits for them, and re-layouts: 9.93 us -> 6.86 us
  matrix products: 13 us -> 14.8 us
    slice x1 -> x0, local copies, waits for them, and re-layouts: 1.84 us -> none  [paired_body(): rows_in = weights[0].reshape(columns, hidden)]
    concatenate x1 -> x0, other arithmetic: 1.55 us -> none  [paired_body(): jnp.concatenate([jnp.transpose(hidden_in), jnp.transpose(hidden_out)], ax...]
    reduce_sum x1, other arithmetic: 0.68 us -> 1.92 us  [paired_body(): cot_sum = cot.astype(jnp.float32).reshape(patches, PATCH, -1).sum(axis=1)]
where the time goes in v2:
time: 113 us; the launch traced here: 112 us
  Pallas kernels  83.5 us (74%)
  matrix products  14.8 us (13%)
  local copies, waits for them, and re-layouts  6.86 us (6%)
  other arithmetic  6.43 us (6%)
    pallas_call x1, Pallas kernels, front(): pl.pallas_call(functools.partial(front_kernel, chips, depth), out_shape=(...  54 us
    pallas_call x1, Pallas kernels, grand_total(): pl.pallas_call(functools.partial(total_kernel, count, shared), out_shape=...  22.9 us
    pallas_call x1, Pallas kernels, row_sum(): pl.pallas_call(swap_kernel, out_shape=jax.ShapeDtypeStruct(x.shape, jnp.f...  6.63 us
    dot_general x8, matrix products, contract(): lax.dot_general(left, right, (((left_dim,), (right_dim,)), ((), ())), pre...  4.12 us

profile of v2, /device:TPU:0, one launch (start us, length us, event | category | flops | bytes accessed | tf_op | source)
XLA Modules:
  0.0 112.5 jit_solution(15649797082843941057)
XLA Ops:
  0.6 0.0 copy-start
  0.6 0.9 fusion.19
  1.6 0.8 convert_element_type.56
  2.4 0.1 copy.28
  2.5 0.7 eq.23
  3.2 0.1 eq.26
  3.3 1.2 %fusion.12 = f32[1024,16]{0,1:T(8,128)S(1)} fusion(f32[8,16]{1,0:T(8,128)} %param.38, s32[1024]{0:T(1024)S(1)} %eq.26), kind=kOutput, calls=%fused_computation.30 | convolution fusion | flops 1581056 | bytes 70144 | tf_op jit(solution)/shard_map/dot_general | solution.py:27
  4.4 0.0 copy-start.11
  4.4 54.0 %front.1 = (bf16[128,1024]{1,0:T(8,128)(2,1)}, f32[128,640]{1,0:T(8,128)}, f32[16,512]{1,0:T(8,128)}, bf16[16,32,1024]{2,1,0:T(8,128)(2,1)}, bf16[16,32,1024]{2,...) custom-call(bf16[128,1024]{1,0:T(8,128)(2,1)} %q_ref.1, bf16[128,1024]{1,0:T(8,128)(2,1)} %k_ref.1, bf16[128,1024]{1,0:T(8,128)(2,1)} %v_ref.1, ...), custom_call_target="tpu_custom_call" | custom-call | tf_op jit(solution)/shard_map/front/pallas_call | solution.py:509
  58.4 0.9 multiply_convert_fusion.3
  59.3 1.9 %convert_reduce_fusion = f32[128,512]{1,0:T(8,128)S(1)} fusion(bf16[128,8,512]{2,1,0:T(8,128)(2,1)} %bitcast.46), kind=kLoop, calls=%fused_computation.7 | loop fusion | flops 983040 | bytes 1310720 | tf_op jit(solution)/shard_map/reduce_sum | solution.py:710
  61.2 0.0 copy-start.7
  61.2 1.1 %fusion.8 = f32[128,512]{1,0:T(8,128)S(1)} fusion(bf16[128,16]{1,0:T(8,128)(2,1)S(1)} %multiply_convert_fusion.3, f32[128,640]{1,0:T(8,128)} %get-tuple-element.12, f32[16,512]{1,0:T(8,128)} %get-tuple-element.13), kind=kOutput, calls=%fused_computation.19 | convolution fusion | flops 2301952 | bytes 561152 | tf_op jit(solution)/shard_map/dot_general | solution.py:688
  62.4 0.0 copy-done
  62.4 0.0 copy-done.11
  62.4 0.6 multiply_reduce_fusion.1
  63.0 0.0 copy-start.5
  63.1 0.0 copy-done.7
  63.1 0.0 copy-start.2
  63.1 0.0 copy-start.10
  63.1 0.2 multiply_convert_fusion
  63.3 0.4 copy-done.5
  63.8 0.4 multiply_convert_fusion.2
  64.1 0.2 copy-done.2
  64.3 0.3 copy-done.10
  64.6 0.0 copy-start.9
  64.6 1.2 %fusion.28 = f32[1024,1024]{1,0:T(8,128)S(1)} fusion(bf16[1024,512]{1,0:T(8,128)(2,1)S(1)} %bitcast.47, bf16[512,1024]{1,0:T(8,128)(2,1)S(1)} %bitcast.54), kind=kOutput, calls=%fused_computation.55 | convolution fusion | flops 1073741824 | bytes 6291456 | tf_op jit(solution)/shard_map/dot_general | solution.py:697
  65.9 0.0 copy-done.9
  65.9 0.0 copy-start.6
  65.9 1.3 %fusion.29 = f32[1024,1024]{1,0:T(8,128)S(1)} fusion(bf16[1024,512]{1,0:T(8,128)(2,1)S(1)} %multiply_convert_fusion, bf16[512,1024]{1,0:T(8,128)(2,1)S(1)} %bitcast.52), kind=kOutput, calls=%fused_computation.56 | convolution fusion | flops 1073741824 | bytes 6291456 | tf_op jit(solution)/shard_map/dot_general | solution.py:694
  67.2 0.0 copy-done.6
  67.2 2.3 %fusion.5 = bf16[1024,1024]{1,0:T(8,128)(2,1)S(1)} fusion(f32[1024,1024]{1,0:T(8,128)S(1)} %fusion.28, f32[1024,1024]{1,0:T(8,128)S(1)} %fusion.29, bf16[1024,16]{0,1:T(8,128)(2,1)S(1)} %get-tuple-element.26, bf16[16,1024]{1,0:T(8,128)(2,1)S(1)} %copy-done.6), kind=kOutput, calls=%fused_computation.6 | convolution fusion | flops 45088768 | bytes 10551296 | tf_op jit(solution)/shard_map/dot_general | solution.py:694
  69.4 0.4 convolution_convert_fusion.1
  69.8 0.7 multiply_convert_fusion.1
  70.5 1.3 %fusion.30 = f32[1024,512]{1,0:T(8,128)S(1)} fusion(bf16[1024,1024]{1,0:T(8,128)(2,1)S(1)} %fusion.5, bf16[512,1024]{1,0:T(8,128)(2,1)S(1)} %bitcast.53), kind=kOutput, calls=%fused_computation.57 | convolution fusion | flops 1073741824 | bytes 5242880 | tf_op jit(solution)/shard_map/dot_general | solution.py:18
  71.8 0.2 convolution_convert_fusion.3
  72.0 0.6 convolution_convert_fusion.4
  72.6 0.6 multiply_reduce_fusion
  73.2 0.0 copy-start.4
  73.3 0.0 copy-start.3
  73.3 0.0 copy-start.1
  73.3 1.6 %bitcast_reduce_fusion.x_ref = bf16[128,512]{1,0:T(8,128)(2,1)} fusion(f32[1024,512]{1,0:T(8,128)S(1)} %get-tuple-element.31, f32[1024,512]{1,0:T(8,128)S(1)} %get-tuple-element.25, f32[1024]{0:T(1024)S(1)} %broadcast_multiply_fusion, f32[1024]{0:T(1024)S(1)} %add_rsqrt_fusion), kind=kLoop, calls=%fused_computation.8 | loop fusion | flops 3080192 | bytes 4333568 | tf_op jit(solution)/shard_map/reduce_sum | solution.py:709
  74.8 0.0 copy-start.8
  74.8 6.6 %row_sum.1 = f32[128,512]{1,0:T(8,128)} custom-call(bf16[128,512]{1,0:T(8,128)(2,1)} %bitcast_reduce_fusion.x_ref), custom_call_target="tpu_custom_call" | custom-call | tf_op jit(solution)/shard_map/row_sum/pallas_call | solution.py:565
  81.5 1.0 add_convert_fusion
  82.5 0.0 copy-done.4
  82.5 0.1 fusion.23
  82.6 0.0 copy-done.3
  82.6 0.2 convolution_convert_fusion.2
  82.8 0.0 copy-done.1
  82.8 0.6 fusion.9
  83.4 0.1 copy.29
  83.5 0.0 copy-done.8
  83.5 1.1 fusion.10
  84.6 0.1 maximum_maximum_fusion
  84.7 0.7 convert_element_type.71.g_ref
  85.4 22.9 %grand_total.1 = f32[16,16,256]{2,1,0:T(8,128)} custom-call(bf16[16,16,256]{2,1,0:T(8,128)(2,1)} %convert_element_type.71.g_ref), custom_call_target="tpu_custom_call" | custom-call | tf_op jit(solution)/shard_map/grand_total/pallas_call | solution.py:630
  108.4 1.0 fusion.26
  109.3 0.6 slice.50
  110.0 0.6 fusion.27
  110.6 0.6 slice_bitcast_fusion
  111.2 0.6 slice.44
  111.8 0.6 slice.42
  (4 shorter events, 0.0 us)
Async XLA Ops:
  0.6 61.7 %copy-start = (bf16[256,512]{1,0:T(8,128)(2,1)S(1)}, bf16[256,512]{1,0:T(8,128)(2,1)}, u32[]{:S(2)}) copy-start(bf16[256,512]{1,0:T(8,128)(2,1)} %param.31) | copy-start | bytes 786436
  4.4 57.9 %copy-start.11 = (s32[1024]{0:T(1024)S(1)}, s32[1024]{0:T(1024)}, u32[]{:S(2)}) copy-start(s32[1024]{0:T(1024)} %param.30) | copy-start | bytes 12292
  61.2 1.8 %copy-start.7 = (f32[512]{0:T(512)S(1)}, f32[512]{0:T(512)}, u32[]{:S(2)}) copy-start(f32[512]{0:T(512)} %param.33) | copy-start | bytes 6148
  63.0 0.7 copy-start.5
  63.1 1.2 %copy-start.2 = (bf16[2,512,512]{2,1,0:T(8,128)(2,1)S(1)}, bf16[2,512,512]{2,1,0:T(8,128)(2,1)}, u32[]{:S(2)}) copy-start(bf16[2,512,512]{2,1,0:T(8,128)(2,1)} %get-tuple-element.14) | copy-start | bytes 3145732
  63.1 1.5 %copy-start.10 = (bf16[16,32,1024]{2,1,0:T(8,128)(2,1)S(1)}, bf16[16,32,1024]{2,1,0:T(8,128)(2,1)}, u32[]{:S(2)}) copy-start(bf16[16,32,1024]{2,1,0:T(8,128)(2,1)} %get-tuple-element.15) | copy-start | bytes 3145732
  64.6 1.3 %copy-start.9 = (bf16[16,32,1024]{2,1,0:T(8,128)(2,1)S(1)}, bf16[16,32,1024]{2,1,0:T(8,128)(2,1)}, u32[]{:S(2)}) copy-start(bf16[16,32,1024]{2,1,0:T(8,128)(2,1)} %get-tuple-element.16) | copy-start | bytes 3145732
  65.9 1.3 %copy-start.6 = (bf16[16,1024]{1,0:T(8,128)(2,1)S(1)}, bf16[16,1024]{1,0:T(8,128)(2,1)}, u32[]{:S(2)}) copy-start(bf16[16,1024]{1,0:T(8,128)(2,1)} %param.37) | copy-start | bytes 98308
  73.2 9.2 %copy-start.4 = (f32[16,512]{1,0:T(8,128)S(1)}, f32[16,512]{1,0:T(8,128)}, u32[]{:S(2)}) copy-start(f32[16,512]{1,0:T(8,128)} %get-tuple-element.13) | copy-start | bytes 98308
  73.3 9.4 %copy-start.3 = (bf16[128,1024]{1,0:T(8,128)(2,1)S(1)}, bf16[128,1024]{1,0:T(8,128)(2,1)}, u32[]{:S(2)}) copy-start(bf16[128,1024]{1,0:T(8,128)(2,1)} %get-tuple-element.17) | copy-start | bytes 786436
  73.3 9.5 %copy-start.1 = (bf16[1024,512]{1,0:T(8,128)(2,1)S(1)}, bf16[1024,512]{1,0:T(8,128)(2,1)}, u32[]{:S(2)}) copy-start(bf16[1024,512]{1,0:T(8,128)(2,1)} %lw_ref.1) | copy-start | bytes 3145732
  74.8 8.6 %copy-start.8 = (s32[128]{0:T(128)S(1)}, s32[128]{0:T(128)}, u32[]{:S(2)}) copy-start(s32[128]{0:T(128)} %param.23) | copy-start | bytes 1540
